TPU v7x, 32 devices: a whole 2x2x4 slice. The times are simulated.
32 devices in a mesh: groups: 2 (over x), tp: 16 (over z, y, core).
Axes of the slice: x: 2, y: 2, z: 4, core: 2. Of those that a mesh axis runs over, the one named last changes fastest.
Arguments:
- queries: bfloat16 [4, 4096, 4096], P('groups', 'tp'), parts along dimension 0, may hold values from -162 to 162
- keys: bfloat16 [4, 4096, 2048], P('groups', 'tp'), parts along dimension 0, may hold values from -6 to 6
- values: bfloat16 [4, 4096, 2048], P('groups', 'tp'), parts along dimension 0, may hold values from -6 to 6
- lengths: int32 [4], P('groups'), parts along dimension 0, may hold values from 1024 to 4096
Outputs:
- attended: bfloat16 [4, 4096, 4096], P('groups', 'tp'), parts along dimension 0
There are 2 independent parts, one for each index of `groups`. A program takes and returns all parts, laid end to end along the dimension named above; each array names one. Nothing has to cross between parts.
All inputs are finite; a program needn't handle non-finite values.
Results may differ from a plain program's by a relative error of at most 0.0085.
Values may be sent and summed in bfloat16 or wider, within the bound.
A program may use at most 256 MiB of HBM per device.

v0:
```python
import functools
import math

import jax
import jax.numpy as jnp
from jax import lax
from jax.experimental import pallas as pl
from jax.experimental.pallas import tpu as pltpu
from jax.sharding import PartitionSpec as P

HEADS = 32
KVH = 16
HD = 128
GROUP = HEADS // KVH

SOFT_CAP = 50.0
SCORE_SCALE = 1.0 / (math.sqrt(144.0) * SOFT_CAP)
EXP_SCALE = SOFT_CAP * math.log2(math.e)

LEVELS = 4
PLAN = ((1, 1, 1, 1), (0, 0, 2, 2), (0, 0, 2, 2), (0, 0, 3, 3))
MESH = pl.DeviceIdType.MESH


def tasks_of(level):
    tasks = []
    for k, row in enumerate(PLAN):
        at = [z for z in range(LEVELS) if row[z] == level]
        if at:
            tasks.append((k, at))
    return tasks


def layout():
    place, items = {}, []
    key_rows, query_rows, slots = 0, 0, 0
    for level in range(LEVELS):
        key_at, query_at, listed = 0, 0, []
        for slot, (k, at) in enumerate(tasks_of(level)):
            place[level, k] = (slot, key_at, query_at - at[0])
            seen = 0
            for z in at:
                listed.append((k, z, slot, key_at, query_at - at[0], seen))
                seen = z + 1
            key_at += at[-1] + 1
            query_at += len(at)
            slots = max(slots, slot + 1)
        key_rows, query_rows = max(key_rows, key_at), max(query_rows, query_at)
        items.append(listed)
    return place, items, key_rows, query_rows, slots


def pick(values, index):
    if all(v == values[0] for v in values):
        return values[0]
    result = jnp.int32(values[-1])
    for n in reversed(range(len(values) - 1)):
        result = jnp.where(index == n, values[n], result)
    return result


def pick_item(items, field, level, index):
    rows = [[item[field] for item in listed] for listed in items]
    most = max(len(row) for row in rows)
    columns = [pick([row[min(n, len(row) - 1)] for row in rows], level) for n in range(most)]
    result = columns[-1]
    for n in reversed(range(most - 1)):
        result = jnp.where(index == n, columns[n], result)
    return result


def fused_kernel(
    seqs,
    devices,
    length_ref,
    query_ref,
    key_ref,
    value_ref,
    out_ref,
    key_all,
    value_ext,
    query_all,
    mixed_all,
    total_ref,
    arrived,
    sent_own,
    sent_far,
    sent_out,
    returned,
):
    place, items, _, _, _ = layout()
    per = devices // LEVELS
    rows = query_ref.shape[1]
    part = per * rows
    span = min(512, part)
    size = GROUP * HD
    me = lax.axis_index("tp")
    level, lane = me // per, me % per

    barrier = pltpu.get_barrier_semaphore()
    for d in range(1, devices):
        pl.semaphore_signal(
            barrier, inc=1, device_id={"tp": lax.rem(me + d, devices)}, device_id_type=MESH
        )
    pl.semaphore_wait(barrier, devices - 1)

    def send(source, target, sent, landed, to):
        @pl.when(to == me)
        def _():
            pltpu.make_async_copy(source, target, landed).start()

        @pl.when(to != me)
        def _():
            pltpu.make_async_remote_copy(
                src_ref=source,
                dst_ref=target,
                send_sem=sent,
                recv_sem=landed,
                device_id={"tp": to},
                device_id_type=MESH,
            ).start()

    def tile(x, width):
        return pl.ds(pl.multiple_of(x * width, width), width)

    def send_pair(s, k, head, to, at, sent):
        slot, key_at = at
        target = tile(key_at * per + me, rows)
        landed = arrived.at[s, slot, level]
        send(key_ref.at[s, :, tile(head, HD)], key_all.at[s, target], sent, landed, to)
        send(
            value_ref.at[s, :, tile(head, HD)],
            value_ext.at[s, target, pl.ds(0, HD)],
            sent,
            landed,
            to,
        )

    def far_levels(k):
        far = [sorted({PLAN[k][q] for q in range(z, LEVELS)} - {PLAN[k][z]}) for z in range(LEVELS)]
        most = max(len(f) for f in far)
        return [[f[n] if n < len(f) else -1 for f in far] for n in range(most)]

    def at_levels(k, to):
        held = [place.get((to[z], k), (0, 0, 0)) for z in range(LEVELS)]
        return [pick([h[n] for h in held], level) for n in range(3)]

    for s in range(seqs):
        for k in range(len(PLAN)):

            def spread(step, carry, s=s, k=k):
                other = lax.rem(lane + step, per)
                head = k * per + other
                for n, to in enumerate(far_levels(k)):
                    slot, key_at, _ = at_levels(k, to)
                    goes = pick(to, level)

                    @pl.when(goes >= 0)
                    def _():
                        send_pair(s, k, head, goes * per + other, (slot, key_at), sent_far.at[n, s, head])

                slot, key_at, query_at = at_levels(k, PLAN[k])
                dest = pick(PLAN[k], level) * per + other
                send(
                    query_ref.at[s, :, tile(head, size)],
                    query_all.at[s, tile(query_at * per + me, rows)],
                    sent_own.at[s, head],
                    arrived.at[s, slot, level],
                    dest,
                )
                send_pair(s, k, head, dest, (slot, key_at), sent_own.at[s, head])
                return carry

            lax.fori_loop(0, per, spread, 0)

    def wait(ref, sem):
        pltpu.make_async_copy(ref, ref, sem).wait()

    counts = [len(listed) for listed in items]
    blocks = pick(counts, level) * per

    def block_info(index):
        s, rest = index // blocks, index % blocks
        item, j = rest // per, rest % per
        k, z, slot, key_at, query_at, seen = (
            pick_item(items, field, level, item) for field in range(6)
        )
        return s, k, z, slot, key_at, query_at, seen, j

    def return_block(index):
        s, k, z, _, _, query_at, _, j = block_info(index)
        at = z * per + j
        send(
            mixed_all.at[s, tile(query_at * per + at, rows)],
            out_ref.at[s, :, tile(k * per + lane, size)],
            sent_out.at[index],
            returned,
            at,
        )

    def attend(index, carry):
        s, k, z, slot, key_at, query_at, seen, j = block_info(index)
        valid = length_ref[s]
        key_base = key_at * part

        @pl.when(j == 0)
        def _():
            def take(source, carry):
                has_query = functools.reduce(
                    jnp.logical_or,
                    [
                        (k == c) & (source == q) & (level == PLAN[c][q])
                        for c in range(len(PLAN))
                        for q in range(LEVELS)
                    ],
                )

                @pl.when(has_query)
                def _():
                    wait(query_all.at[0, pl.ds(0, 2 * part)], arrived.at[s, slot, source])

                @pl.when(jnp.logical_not(has_query))
                def _():
                    wait(query_all.at[0, pl.ds(0, part)], arrived.at[s, slot, source])

                def extend(n, carry):
                    first = pl.multiple_of(source * part + n * rows, rows)
                    held = pl.ds(pl.multiple_of(key_base + first, rows), rows)
                    pos = first + lax.broadcasted_iota(jnp.int32, (rows, 2 * HD), 0)
                    block = value_ext[s, held, :HD].astype(jnp.float32)
                    block = jnp.concatenate([block, jnp.ones_like(block)], axis=1)
                    value_ext[s, held, :] = jnp.where(pos < valid, block, 0.0).astype(jnp.bfloat16)
                    return carry

                lax.fori_loop(0, per, extend, 0)
                return carry

            lax.fori_loop(seen, z + 1, take, 0)

        start = (z * per + j) * rows
        asked = tile(query_at * per + z * per + j, rows)
        block_q = jnp.concatenate(
            [query_all[s, asked, h * HD : (h + 1) * HD] for h in range(GROUP)], axis=0
        )
        total_ref[...] = jnp.zeros_like(total_ref)

        def step(block, masked):
            first = pl.multiple_of(block * span, span)
            held = pl.ds(pl.multiple_of(key_base + first, span), span)
            score = lax.dot_general(
                block_q,
                key_all[s, held, :],
                (((1,), (1,)), ((), ())),
                preferred_element_type=jnp.float32,
            )
            weight = jnp.exp2(jnp.tanh(score * SCORE_SCALE) * EXP_SCALE)
            if masked:
                shape = (rows, span)
                allowed = first + lax.broadcasted_iota(
                    jnp.int32, shape, 1
                ) <= start + lax.broadcasted_iota(jnp.int32, shape, 0)
                weight = jnp.concatenate(
                    [
                        jnp.where(allowed, weight[h * rows : (h + 1) * rows], 0.0)
                        for h in range(GROUP)
                    ],
                    axis=0,
                )
            total_ref[...] += jnp.dot(
                weight.astype(jnp.bfloat16),
                value_ext[s, held, :],
                preferred_element_type=jnp.float32,
            )

        def plain(block, carry):
            step(block, False)
            return carry

        full = start // span
        lax.fori_loop(0, full, plain, 0)
        step(full, True)

        live = start + lax.broadcasted_iota(jnp.int32, (rows, HD), 0) < valid
        for h in range(GROUP):
            at = slice(h * rows, (h + 1) * rows)
            mixed = total_ref[at, :HD] / total_ref[at, HD:]
            mixed_all[s, asked, h * HD : (h + 1) * HD] = jnp.where(live, mixed, 0.0).astype(
                jnp.bfloat16
            )

        @pl.when(index > 0)
        def _():
            return_block(index - 1)

        return carry

    lax.fori_loop(0, seqs * blocks, attend, 0)

    for s in range(seqs):
        for k in range(len(PLAN)):

            def settle(other, carry, s=s, k=k):
                head = k * per + other
                for n, to in enumerate(far_levels(k)):

                    @pl.when(pick(to, level) >= 0)
                    def _():
                        wait(query_all.at[0, pl.ds(0, rows)], sent_far.at[n, s, head])

                @pl.when(pick(PLAN[k], level) * per + other != me)
                def _():
                    wait(query_all.at[0, pl.ds(0, 2 * rows)], sent_own.at[s, head])

                return carry

            lax.fori_loop(0, per, settle, 0)

    return_block(seqs * blocks - 1)

    def settle_out(index, carry):
        _, _, z, _, _, _, _, j = block_info(index)

        @pl.when(z * per + j != me)
        def _():
            wait(mixed_all.at[0, pl.ds(0, rows)], sent_out.at[index])

        return carry

    lax.fori_loop(0, seqs * blocks, settle_out, 0)
    wait(out_ref, returned)


def fused(queries, keys, values, lengths):
    seqs, rows, width = queries.shape
    devices = lax.axis_size("tp")
    per = devices // LEVELS
    part = per * rows
    _, items, key_levels, query_levels, slots = layout()
    far = max(LEVELS - 1, 1)
    most = seqs * per * max(len(listed) for listed in items)
    anywhere = pl.BlockSpec(memory_space=pl.ANY)
    count = devices * rows
    return pl.pallas_call(
        functools.partial(fused_kernel, seqs, devices),
        in_specs=[pl.BlockSpec(memory_space=pltpu.SMEM), anywhere, anywhere, anywhere],
        out_specs=anywhere,
        out_shape=jax.ShapeDtypeStruct((seqs, rows, width), jnp.bfloat16),
        scratch_shapes=[
            pltpu.VMEM((seqs, key_levels * part, HD), jnp.bfloat16),
            pltpu.VMEM((seqs, key_levels * part, 2 * HD), jnp.bfloat16),
            pltpu.VMEM((seqs, query_levels * part, GROUP * HD), jnp.bfloat16),
            pltpu.VMEM((seqs, query_levels * part, GROUP * HD), jnp.bfloat16),
            pltpu.VMEM((GROUP * rows, 2 * HD), jnp.float32),
            pltpu.SemaphoreType.DMA((seqs, slots, LEVELS)),
            pltpu.SemaphoreType.DMA((seqs, KVH)),
            pltpu.SemaphoreType.DMA((far, seqs, KVH)),
            pltpu.SemaphoreType.DMA((most,)),
            pltpu.SemaphoreType.DMA,
        ],
        cost_estimate=pl.CostEstimate(
            flops=4 * seqs * HEADS * count * count * HD // devices,
            bytes_accessed=8 * seqs * rows * width,
            transcendentals=seqs * HEADS * count * count // devices,
        ),
        compiler_params=pltpu.CompilerParams(
            collective_id=0, has_side_effects=True, vmem_limit_bytes=60 * 1024 * 1024
        ),
    )(lengths, queries, keys, values)


def fused_fits(devices):
    return devices % LEVELS == 0 and KVH == devices


def attend_block(
    heads,
    width,
    span,
    start,
    valid,
    query_ref,
    at_q,
    key_all,
    value_ext,
    out_ref,
    at_o,
    total_ref,
):
    @pl.when(start >= valid)
    def _():
        out_ref[...] = jnp.zeros_like(out_ref)

    @pl.when(start < valid)
    def _():
        block_q = jnp.concatenate(
            [query_ref[at_q + (slice(None), slice(h * HD, (h + 1) * HD))] for h in range(heads)],
            axis=0,
        )
        total_ref[...] = jnp.zeros_like(total_ref)

        def step(block, masked):
            first = pl.multiple_of(block * span, span)
            held = pl.ds(first, span)
            score = lax.dot_general(
                block_q,
                key_all[held, :],
                (((1,), (1,)), ((), ())),
                preferred_element_type=jnp.float32,
            )
            weight = jnp.exp2(jnp.tanh(score * SCORE_SCALE) * EXP_SCALE)
            if masked:
                shape = (width, span)
                key_pos = first + lax.broadcasted_iota(jnp.int32, shape, 1)
                query_pos = start + lax.broadcasted_iota(jnp.int32, shape, 0)
                allowed = (key_pos <= query_pos) & (key_pos < valid)
                weight = jnp.concatenate(
                    [
                        jnp.where(allowed, weight[h * width : (h + 1) * width], 0.0)
                        for h in range(heads)
                    ],
                    axis=0,
                )
            total_ref[...] += jnp.dot(
                weight.astype(jnp.bfloat16),
                value_ext[held, :],
                preferred_element_type=jnp.float32,
            )

        full = jnp.minimum(start + 1, valid) // span
        stop = (jnp.minimum(start + width, valid) + span - 1) // span

        def plain(block, carry):
            step(block, False)
            return carry

        def edge(block, carry):
            step(block, True)
            return carry

        lax.fori_loop(0, full, plain, 0)
        lax.fori_loop(full, stop, edge, 0)
        live = start + lax.broadcasted_iota(jnp.int32, (width, HD), 0) < valid
        for h in range(heads):
            part = slice(h * width, (h + 1) * width)
            mixed = total_ref[part, :HD] / total_ref[part, HD:]
            out_ref[at_o + (slice(None), slice(h * HD, (h + 1) * HD))] = jnp.where(
                live, mixed, 0.0
            ).astype(jnp.bfloat16)


def attend_kernel(heads, width, span, length_ref, packed_ref, out_ref, key_all, value_ext, total_ref):
    index = pl.program_id(0)
    count = packed_ref.shape[0]
    start = pl.multiple_of(index * width, width)

    @pl.when(index == 0)
    def _():
        key_all[...] = packed_ref[:, heads * HD : (heads + 1) * HD]
        value_ext[:, :HD] = packed_ref[:, (heads + 1) * HD :]
        value_ext[:, HD:] = jnp.ones((count, HD), jnp.bfloat16)

    query = packed_ref.at[pl.ds(start, width)]
    attend_block(
        heads, width, span, start, length_ref[0], query, (), key_all, value_ext, out_ref, (), total_ref
    )


def attend(packed, valid, heads):
    count = packed.shape[0]
    width = min(256, count)
    span = min(512, count)
    return pl.pallas_call(
        functools.partial(attend_kernel, heads, width, span),
        grid_spec=pltpu.PrefetchScalarGridSpec(
            num_scalar_prefetch=1,
            grid=(count // width,),
            in_specs=[pl.BlockSpec((count, (heads + 2) * HD), lambda i, _: (0, 0))],
            out_specs=pl.BlockSpec((width, heads * HD), lambda i, _: (i, 0)),
            scratch_shapes=[
                pltpu.VMEM((count, HD), jnp.bfloat16),
                pltpu.VMEM((count, 2 * HD), jnp.bfloat16),
                pltpu.VMEM((heads * width, 2 * HD), jnp.float32),
            ],
        ),
        out_shape=jax.ShapeDtypeStruct((count, heads * HD), jnp.bfloat16),
        cost_estimate=pl.CostEstimate(
            flops=4 * heads * count * count * HD,
            bytes_accessed=2 * count * HD * (2 * heads + 2),
            transcendentals=heads * count * count,
        ),
        compiler_params=pltpu.CompilerParams(
            dimension_semantics=("arbitrary",), vmem_limit_bytes=40 * 1024 * 1024
        ),
    )(valid, packed)


def exchange(array):
    return lax.all_to_all(
        array, "tp", split_axis=0, concat_axis=0, tiled=True
    )


def per_device(queries, keys, values, lengths):
    seqs, rows, _ = queries.shape
    devices = lax.axis_size("tp")
    count = devices * rows
    if fused_fits(devices):
        return fused(queries, keys, values, lengths)

    pairs = seqs * HEADS
    owned = pairs // devices
    heads_q = queries.reshape(seqs, rows, HEADS, HD)
    heads_k = jnp.repeat(keys.reshape(seqs, rows, KVH, HD), GROUP, axis=2)
    heads_v = jnp.repeat(values.reshape(seqs, rows, KVH, HD), GROUP, axis=2)
    packed = jnp.concatenate([heads_q, heads_k, heads_v], axis=3)
    packed = packed.transpose(0, 2, 1, 3).reshape(devices, owned * rows, 3 * HD)
    gathered = exchange(packed).reshape(devices, owned, rows, 3 * HD)
    outs = []
    for o in range(owned):
        seq = (lax.axis_index("tp") * owned + o) // HEADS
        valid = jnp.sum(jnp.where(jnp.arange(seqs) == seq, lengths, 0))[None]
        outs.append(attend(gathered[:, o].reshape(count, 3 * HD), valid, 1))
    output = jnp.stack(outs).reshape(owned, devices, rows, HD).transpose(1, 0, 2, 3)
    returned = exchange(output.reshape(devices, owned * rows, HD))
    return (
        returned.reshape(seqs, HEADS, rows, HD)
        .transpose(0, 2, 1, 3)
        .reshape(seqs, rows, HEADS * HD)
    )


def solution(mesh):
    placed = (
        P("groups", "tp", None),
        P("groups", "tp", None),
        P("groups", "tp", None),
        P("groups"),
    )
    return jax.shard_map(
        per_device, mesh=mesh, in_specs=placed, out_specs=P("groups", "tp", None), check_vma=False
    )
```

profile of v0, /device:TPU:29, one launch (start us, length us, event | category | flops | bytes accessed | tf_op | source)
XLA Modules:
  0.0 198.6 jit_solution(10900270759199906653)
XLA Ops:
  0.0 193.9 %shard_map.46 = bf16[2,256,4096]{2,1,0:T(8,128)(2,1)} custom-call(s32[2]{0:T(128)} %length_ref.1, bf16[2,256,4096]{2,1,0:T(8,128)(2,1)} %query_ref.1, bf16[2,256,2048]{2,1,0:T(8,128)(2,1)} %key_ref.1, bf16[2,256,2048]{2,1,0:T(8,128)(2,1)} %value_ref.1), custom_call_target="tpu_custom_call" | custom-call | flops 34359738368 | bytes 16777216 | tf_op jit(solution)/shard_map/pallas_call | solution.py:343
  193.9 4.7 %copy.6 = bf16[2,256,4096]{2,1,0:T(8,128)(2,1)} copy(bf16[2,256,4096]{2,1,0:T(8,128)(2,1)} %shard_map.46) | data formatting | bytes 8388608
where the time goes:
time: 200 us; the launch traced here: 199 us
  Pallas kernels  194 us (97%)
  local copies, waits for them, and re-layouts  4.7 us (2%)
    pallas_call x1, Pallas kernels, fused(): pl.pallas_call(functools.partial(fused_kernel, seqs, devices), in_specs=[...  194 us
    unnamed x1, local copies, waits for them, and re-layouts  4.7 us

commit v1 on v0

--- a/solution.py
+++ b/solution.py
@@ -17,41 +17,89 @@
 SCORE_SCALE = 1.0 / (math.sqrt(144.0) * SOFT_CAP)
 EXP_SCALE = SOFT_CAP * math.log2(math.e)
 
-LEVELS = 4
-PLAN = ((1, 1, 1, 1), (0, 0, 2, 2), (0, 0, 2, 2), (0, 0, 3, 3))
+LEVELS = 8
+PLANS = (
+    (
+        "22222222",
+        "33333333",
+        "00004444",
+        "11115555",
+        "00004444",
+        "11115555",
+        "00006666",
+        "11117777",
+    ),
+    (
+        "22222222",
+        "33333333",
+        "00004444",
+        "11115555",
+        "00004444",
+        "11115555",
+        "00006666",
+        "11117777",
+    ),
+)
 MESH = pl.DeviceIdType.MESH
 
 
-def tasks_of(level):
-    tasks = []
-    for k, row in enumerate(PLAN):
-        at = [z for z in range(LEVELS) if row[z] == level]
-        if at:
-            tasks.append((k, at))
-    return tasks
-
-
-def layout():
-    place, items = {}, []
-    key_rows, query_rows, slots = 0, 0, 0
-    for level in range(LEVELS):
-        key_at, query_at, listed = 0, 0, []
-        for slot, (k, at) in enumerate(tasks_of(level)):
-            place[level, k] = (slot, key_at, query_at - at[0])
-            seen = 0
-            for z in at:
-                listed.append((k, z, slot, key_at, query_at - at[0], seen))
-                seen = z + 1
-            key_at += at[-1] + 1
-            query_at += len(at)
-            slots = max(slots, slot + 1)
-        key_rows, query_rows = max(key_rows, key_at), max(query_rows, query_at)
-        items.append(listed)
-    return place, items, key_rows, query_rows, slots
+class Layout:
+    def __init__(self, plans):
+        self.owner = [[[int(z) for z in row] for row in plan] for plan in plans]
+        self.key_at, self.query_at, self.slot = {}, {}, {}
+        self.items = [[] for _ in range(LEVELS)]
+        self.key_levels = self.query_levels = self.slots = 0
+        for level in range(LEVELS):
+            for s, plan in enumerate(self.owner):
+                keys = queries = slots = 0
+                for k, row in enumerate(plan):
+                    asked = [z for z, owner in enumerate(row) if owner == level]
+                    if not asked:
+                        continue
+                    self.key_at[s, k, level] = keys
+                    self.slot[s, k, level] = slots
+                    seen = 0
+                    for z in asked:
+                        self.query_at[s, k, z] = queries
+                        self.items[level].append((s, k, z, slots, keys, queries, seen, asked))
+                        queries += 1
+                        seen = z + 1
+                    keys += asked[-1] + 1
+                    slots += 1
+                self.key_levels = max(self.key_levels, keys)
+                self.query_levels = max(self.query_levels, queries)
+                self.slots = max(self.slots, slots)
+
+    def sends(self, level):
+        listed = []
+        for s, plan in enumerate(self.owner):
+            for k, row in enumerate(plan):
+                if level >= len(row):
+                    continue
+                for to in sorted(set(row[level:])):
+                    query = 1 + self.query_at[s, k, level] if to == row[level] else 0
+                    listed.append((s, k, to, query, self.slot[s, k, to], self.key_at[s, k, to]))
+
+        def rank(sent):
+            s, k, to, query, _, _ = sent
+            return (s, k // 2)
+
+        ordered = []
+        for group in sorted({rank(sent) for sent in listed}):
+            near = [x for x in listed if rank(x) == group and (x[2] ^ level) & 1 == 0]
+            across = [x for x in listed if rank(x) == group and (x[2] ^ level) & 1 == 1]
+            near.sort(key=lambda x: x[3] > 0)
+            across.sort(key=lambda x: x[3] > 0)
+            for n in range(max(len(near), len(across))):
+                ordered += near[n : n + 1] + across[n : n + 1]
+        return ordered
+
+    def active(self, s):
+        return len(self.owner[s][0])
 
 
 def pick(values, index):
-    if all(v == values[0] for v in values):
+    if all(isinstance(v, int) and v == values[0] for v in values):
         return values[0]
     result = jnp.int32(values[-1])
     for n in reversed(range(len(values) - 1)):
@@ -59,18 +107,22 @@
     return result
 
 
-def pick_item(items, field, level, index):
-    rows = [[item[field] for item in listed] for listed in items]
-    most = max(len(row) for row in rows)
-    columns = [pick([row[min(n, len(row) - 1)] for row in rows], level) for n in range(most)]
-    result = columns[-1]
-    for n in reversed(range(most - 1)):
-        result = jnp.where(index == n, columns[n], result)
-    return result
+def columns_of(items, code, level):
+    most = max(len(listed) for listed in items)
+    codes = [[code(item) for item in listed] or [0] for listed in items]
+    return [pick([row[min(n, len(row) - 1)] for row in codes], level) for n in range(most)]
+
+
+def pack_fields(fields, bits):
+    return sum(field << (bits * n) for n, field in enumerate(fields))
+
+
+def split_fields(code, bits, count):
+    return [(code >> (bits * n)) & ((1 << bits) - 1) for n in range(count)]
 
 
 def fused_kernel(
-    seqs,
+    plans,
     devices,
     length_ref,
     query_ref,
@@ -82,13 +134,14 @@
     query_all,
     mixed_all,
     total_ref,
+    blank,
     arrived,
-    sent_own,
-    sent_far,
+    sent_in,
     sent_out,
     returned,
 ):
-    place, items, _, _, _ = layout()
+    layout = Layout(plans)
+    seqs = len(plans)
     per = devices // LEVELS
     rows = query_ref.shape[1]
     part = per * rows
@@ -123,103 +176,99 @@
     def tile(x, width):
         return pl.ds(pl.multiple_of(x * width, width), width)
 
-    def send_pair(s, k, head, to, at, sent):
-        slot, key_at = at
+    def wait(ref, sem):
+        pltpu.make_async_copy(ref, ref, sem).wait()
+
+    sends = [layout.sends(z) for z in range(LEVELS)]
+    groups = pick([len(listed) for listed in sends], level) * per
+
+    send_codes = columns_of(sends, lambda i: pack_fields((i[0], i[1], i[2], i[4]), 6), level)
+    send_rows = columns_of(sends, lambda i: pack_fields((i[3], i[5]), 6), level)
+
+    def send_info(index):
+        n, step = index // per, index % per
+        n = jnp.where((n ^ (lane & 1)) * per < groups, n ^ (lane & 1), n)
+        s, k, to, slot = split_fields(pick(send_codes, n), 6, 4)
+        query, key_at = split_fields(pick(send_rows, n), 6, 2)
+        other = lax.rem(lane + step, per)
+        return s, k * per + other, to * per + other, query, slot, key_at
+
+    def spread(index, carry):
+        s, head, dest, query, slot, key_at = send_info(index)
+        landed, sent = arrived.at[s, slot, level], sent_in.at[index]
         target = tile(key_at * per + me, rows)
-        landed = arrived.at[s, slot, level]
-        send(key_ref.at[s, :, tile(head, HD)], key_all.at[s, target], sent, landed, to)
+
+        @pl.when(query > 0)
+        def _():
+            target_q = tile((query - 1) * per + lane, rows)
+            send(
+                query_ref.at[s, :, tile(head, size)],
+                query_all.at[s, target_q],
+                sent,
+                landed,
+                dest,
+            )
+
+        send(key_ref.at[s, :, tile(head, HD)], key_all.at[s, target], sent, landed, dest)
         send(
             value_ref.at[s, :, tile(head, HD)],
             value_ext.at[s, target, pl.ds(0, HD)],
             sent,
             landed,
-            to,
+            dest,
         )
-
-    def far_levels(k):
-        far = [sorted({PLAN[k][q] for q in range(z, LEVELS)} - {PLAN[k][z]}) for z in range(LEVELS)]
-        most = max(len(f) for f in far)
-        return [[f[n] if n < len(f) else -1 for f in far] for n in range(most)]
-
-    def at_levels(k, to):
-        held = [place.get((to[z], k), (0, 0, 0)) for z in range(LEVELS)]
-        return [pick([h[n] for h in held], level) for n in range(3)]
-
-    for s in range(seqs):
-        for k in range(len(PLAN)):
-
-            def spread(step, carry, s=s, k=k):
-                other = lax.rem(lane + step, per)
-                head = k * per + other
-                for n, to in enumerate(far_levels(k)):
-                    slot, key_at, _ = at_levels(k, to)
-                    goes = pick(to, level)
-
-                    @pl.when(goes >= 0)
-                    def _():
-                        send_pair(s, k, head, goes * per + other, (slot, key_at), sent_far.at[n, s, head])
-
-                slot, key_at, query_at = at_levels(k, PLAN[k])
-                dest = pick(PLAN[k], level) * per + other
-                send(
-                    query_ref.at[s, :, tile(head, size)],
-                    query_all.at[s, tile(query_at * per + me, rows)],
-                    sent_own.at[s, head],
-                    arrived.at[s, slot, level],
-                    dest,
-                )
-                send_pair(s, k, head, dest, (slot, key_at), sent_own.at[s, head])
-                return carry
-
-            lax.fori_loop(0, per, spread, 0)
-
-    def wait(ref, sem):
-        pltpu.make_async_copy(ref, ref, sem).wait()
-
-    counts = [len(listed) for listed in items]
-    blocks = pick(counts, level) * per
+        return carry
+
+    lax.fori_loop(0, groups, spread, 0)
+
+    idle = [s for s in range(seqs) if layout.active(s) < LEVELS]
+    if idle:
+        blank[...] = jnp.zeros_like(blank)
+        for s in idle:
+
+            @pl.when(level >= layout.active(s))
+            def _(s=s):
+                pltpu.make_async_copy(blank, out_ref.at[s], returned).start()
+
+    blocks = pick([len(listed) * per for listed in layout.items], level)
+
+    item_codes = columns_of(layout.items, lambda i: pack_fields(i[:5], 6), level)
+    item_rows = columns_of(
+        layout.items,
+        lambda i: pack_fields((i[5], i[6]), 6) + (sum(1 << z for z in i[7]) << 12),
+        level,
+    )
 
     def block_info(index):
-        s, rest = index // blocks, index % blocks
-        item, j = rest // per, rest % per
-        k, z, slot, key_at, query_at, seen = (
-            pick_item(items, field, level, item) for field in range(6)
-        )
-        return s, k, z, slot, key_at, query_at, seen, j
+        item, j = index // per, index % per
+        code, more = pick(item_codes, item), pick(item_rows, item)
+        return *split_fields(code, 6, 5), *split_fields(more, 6, 2), more >> 12, j
 
     def return_block(index):
-        s, k, z, _, _, query_at, _, j = block_info(index)
-        at = z * per + j
+        s, k, z, _, _, query_at, _, _, j = block_info(index)
         send(
-            mixed_all.at[s, tile(query_at * per + at, rows)],
+            mixed_all.at[s, tile(query_at * per + j, rows)],
             out_ref.at[s, :, tile(k * per + lane, size)],
             sent_out.at[index],
             returned,
-            at,
+            z * per + j,
         )
 
     def attend(index, carry):
-        s, k, z, slot, key_at, query_at, seen, j = block_info(index)
+        s, k, z, slot, key_at, query_at, seen, asked, j = block_info(index)
         valid = length_ref[s]
         key_base = key_at * part
 
         @pl.when(j == 0)
         def _():
             def take(source, carry):
-                has_query = functools.reduce(
-                    jnp.logical_or,
-                    [
-                        (k == c) & (source == q) & (level == PLAN[c][q])
-                        for c in range(len(PLAN))
-                        for q in range(LEVELS)
-                    ],
-                )
-
-                @pl.when(has_query)
+                asks = (asked >> source) & 1
+
+                @pl.when(asks == 1)
                 def _():
                     wait(query_all.at[0, pl.ds(0, 2 * part)], arrived.at[s, slot, source])
 
-                @pl.when(jnp.logical_not(has_query))
+                @pl.when(asks == 0)
                 def _():
                     wait(query_all.at[0, pl.ds(0, part)], arrived.at[s, slot, source])
 
@@ -238,9 +287,9 @@
             lax.fori_loop(seen, z + 1, take, 0)
 
         start = (z * per + j) * rows
-        asked = tile(query_at * per + z * per + j, rows)
+        held_q = tile(query_at * per + j, rows)
         block_q = jnp.concatenate(
-            [query_all[s, asked, h * HD : (h + 1) * HD] for h in range(GROUP)], axis=0
+            [query_all[s, held_q, h * HD : (h + 1) * HD] for h in range(GROUP)], axis=0
         )
         total_ref[...] = jnp.zeros_like(total_ref)
 
@@ -284,7 +333,7 @@
         for h in range(GROUP):
             at = slice(h * rows, (h + 1) * rows)
             mixed = total_ref[at, :HD] / total_ref[at, HD:]
-            mixed_all[s, asked, h * HD : (h + 1) * HD] = jnp.where(live, mixed, 0.0).astype(
+            mixed_all[s, held_q, h * HD : (h + 1) * HD] = jnp.where(live, mixed, 0.0).astype(
                 jnp.bfloat16
             )
 
@@ -294,31 +343,29 @@
 
         return carry
 
-    lax.fori_loop(0, seqs * blocks, attend, 0)
-
-    for s in range(seqs):
-        for k in range(len(PLAN)):
-
-            def settle(other, carry, s=s, k=k):
-                head = k * per + other
-                for n, to in enumerate(far_levels(k)):
-
-                    @pl.when(pick(to, level) >= 0)
-                    def _():
-                        wait(query_all.at[0, pl.ds(0, rows)], sent_far.at[n, s, head])
-
-                @pl.when(pick(PLAN[k], level) * per + other != me)
-                def _():
-                    wait(query_all.at[0, pl.ds(0, 2 * rows)], sent_own.at[s, head])
-
-                return carry
-
-            lax.fori_loop(0, per, settle, 0)
-
-    return_block(seqs * blocks - 1)
+    lax.fori_loop(0, blocks, attend, 0)
+
+    def settle(index, carry):
+        _, _, dest, query, _, _ = send_info(index)
+
+        @pl.when((dest != me) & (query > 0))
+        def _():
+            wait(query_all.at[0, pl.ds(0, 2 * rows)], sent_in.at[index])
+
+        @pl.when((dest != me) & (query == 0))
+        def _():
+            wait(query_all.at[0, pl.ds(0, rows)], sent_in.at[index])
+
+        return carry
+
+    lax.fori_loop(0, groups, settle, 0)
+
+    @pl.when(blocks > 0)
+    def _():
+        return_block(blocks - 1)
 
     def settle_out(index, carry):
-        _, _, z, _, _, _, _, j = block_info(index)
+        _, _, z, _, _, _, _, _, j = block_info(index)
 
         @pl.when(z * per + j != me)
         def _():
@@ -326,34 +373,33 @@
 
         return carry
 
-    lax.fori_loop(0, seqs * blocks, settle_out, 0)
+    lax.fori_loop(0, blocks, settle_out, 0)
     wait(out_ref, returned)
 
 
-def fused(queries, keys, values, lengths):
+def fused(queries, keys, values, lengths, plans, collective_id):
     seqs, rows, width = queries.shape
     devices = lax.axis_size("tp")
     per = devices // LEVELS
     part = per * rows
-    _, items, key_levels, query_levels, slots = layout()
-    far = max(LEVELS - 1, 1)
-    most = seqs * per * max(len(listed) for listed in items)
+    layout = Layout(plans)
+    most = per * max(len(listed) for listed in layout.items)
     anywhere = pl.BlockSpec(memory_space=pl.ANY)
     count = devices * rows
     return pl.pallas_call(
-        functools.partial(fused_kernel, seqs, devices),
+        functools.partial(fused_kernel, plans, devices),
         in_specs=[pl.BlockSpec(memory_space=pltpu.SMEM), anywhere, anywhere, anywhere],
         out_specs=anywhere,
         out_shape=jax.ShapeDtypeStruct((seqs, rows, width), jnp.bfloat16),
         scratch_shapes=[
-            pltpu.VMEM((seqs, key_levels * part, HD), jnp.bfloat16),
-            pltpu.VMEM((seqs, key_levels * part, 2 * HD), jnp.bfloat16),
-            pltpu.VMEM((seqs, query_levels * part, GROUP * HD), jnp.bfloat16),
-            pltpu.VMEM((seqs, query_levels * part, GROUP * HD), jnp.bfloat16),
+            pltpu.VMEM((seqs, layout.key_levels * part, HD), jnp.bfloat16),
+            pltpu.VMEM((seqs, layout.key_levels * part, 2 * HD), jnp.bfloat16),
+            pltpu.VMEM((seqs, layout.query_levels * part, GROUP * HD), jnp.bfloat16),
+            pltpu.VMEM((seqs, layout.query_levels * part, GROUP * HD), jnp.bfloat16),
             pltpu.VMEM((GROUP * rows, 2 * HD), jnp.float32),
-            pltpu.SemaphoreType.DMA((seqs, slots, LEVELS)),
-            pltpu.SemaphoreType.DMA((seqs, KVH)),
-            pltpu.SemaphoreType.DMA((far, seqs, KVH)),
+            pltpu.VMEM((rows, width), jnp.bfloat16),
+            pltpu.SemaphoreType.DMA((seqs, layout.slots, LEVELS)),
+            pltpu.SemaphoreType.DMA((per * max(len(layout.sends(z)) for z in range(LEVELS)),)),
             pltpu.SemaphoreType.DMA((most,)),
             pltpu.SemaphoreType.DMA,
         ],
@@ -363,13 +409,13 @@
             transcendentals=seqs * HEADS * count * count // devices,
         ),
         compiler_params=pltpu.CompilerParams(
-            collective_id=0, has_side_effects=True, vmem_limit_bytes=60 * 1024 * 1024
+            collective_id=collective_id, has_side_effects=True, vmem_limit_bytes=36 * 1024 * 1024
         ),
-    )(lengths, queries, keys, values)
-
-
-def fused_fits(devices):
-    return devices % LEVELS == 0 and KVH == devices
+    )(lengths, *(pltpu.with_memory_space_constraint(x, pltpu.HBM) for x in (queries, keys, values)))
+
+
+def fused_fits(devices, seqs):
+    return devices % LEVELS == 0 and KVH == devices and seqs == len(PLANS)
 
 
 def attend_block(
@@ -504,8 +550,8 @@
     seqs, rows, _ = queries.shape
     devices = lax.axis_size("tp")
     count = devices * rows
-    if fused_fits(devices):
-        return fused(queries, keys, values, lengths)
+    if fused_fits(devices, seqs):
+        return fused(queries, keys, values, lengths, PLANS, 0)
 
     pairs = seqs * HEADS
     owned = pairs // devices

time: 200 us -> 196 us (0.980)
  local copies, waits for them, and re-layouts: 4.7 us -> 2.67 us
    unnamed x1 -> x3, local copies, waits for them, and re-layouts: 4.7 us -> 2.67 us
where the time goes in v1:
time: 196 us; the launch traced here: 195 us
  Pallas kernels  193 us (98%)
  local copies, waits for them, and re-layouts  2.67 us (1%)
    pallas_call x1, Pallas kernels, fused(): pl.pallas_call(functools.partial(fused_kernel, plans, devices), in_specs=...  193 us

profile of v1, /device:TPU:29, one launch (start us, length us, event | category | flops | bytes accessed | tf_op | source)
XLA Modules:
  0.0 195.5 jit_solution(391683426118670747)
XLA Ops:
  0.0 0.0 copy-start
  0.0 0.7 copy-done
  0.7 192.8 %shard_map.46 = bf16[2,256,4096]{2,1,0:T(8,128)(2,1)S(1)} custom-call(s32[2]{0:T(128)S(1)} %copy-done, bf16[2,256,4096]{2,1,0:T(8,128)(2,1)} %query_ref.1, bf16[2,256,2048]{2,1,0:T(8,128)(2,1)} %key_ref.1, bf16[2,256,2048]{2,1,0:T(8,128)(2,1)} %value_ref.1), custom_call_target="tpu_custom_call" | custom-call | flops 34359738368 | bytes 16777216 | tf_op jit(solution)/shard_map/pallas_call | solution.py:389
  193.4 2.0 %copy.6 = bf16[2,256,4096]{2,1,0:T(8,128)(2,1)} copy(bf16[2,256,4096]{2,1,0:T(8,128)(2,1)S(1)} %shard_map.46) | data formatting | bytes 8388608
Async XLA Ops:
  0.0 0.7 copy-start
